TPU v7x, 64 devices: a 2x2x8 block of a 4x4x8 slice. The times are simulated.
64 devices in a mesh: dp: 8 (over x, y, core), tp: 8 (over z).
Axes of the slice: x: 2, y: 2, z: 8, core: 2. Of those that a mesh axis runs over, the one named last changes fastest.
The devices are a block of a 4x4x8 slice.
Arguments:
- x: bfloat16 [14336, 5120], P(('dp', 'tp')), parts along dimension 0
- w_gate: bfloat16 [5120, 17408], P(None, 'tp')
- w_up: bfloat16 [5120, 17408], P(None, 'tp')
- w_down: bfloat16 [17408, 5120], P('tp')
Outputs:
- output: bfloat16 [14336, 5120], P(('dp', 'tp')), parts along dimension 0
There are 8 independent parts. A program takes and returns all parts, laid end to end along the dimension named above; an argument that names none is the same for every part.
All inputs are finite; a program needn't handle non-finite values.
Results may differ from a plain program's by a relative error of at most 0.016.
Values are sent between devices in bfloat16 or wider.
A program may use at most 768 MiB of HBM per device.

v0:
```python
import jax
import jax.numpy as jnp
from jax import lax
from jax.sharding import PartitionSpec as P


def solution(mesh):
    def step(x, w_gate, w_up, w_down):
        rows = lax.all_gather(x, "tp", axis=0, tiled=True)
        gate = jnp.dot(rows, w_gate, preferred_element_type=jnp.float32)
        up = jnp.dot(rows, w_up, preferred_element_type=jnp.float32)
        hidden = (jax.nn.silu(gate) * up).astype(jnp.bfloat16)
        term = jnp.dot(hidden, w_down, preferred_element_type=jnp.float32).astype(jnp.bfloat16)
        return lax.psum_scatter(term, "tp", scatter_dimension=0, tiled=True)

    return jax.shard_map(
        step,
        mesh=mesh,
        in_specs=(P(("dp", "tp"), None), P(None, "tp"), P(None, "tp"), P("tp", None)),
        out_specs=P(("dp", "tp"), None),
        check_vma=False,
    )
```

profile of v0, /device:TPU:22, one launch (start us, length us, event | category | flops | bytes accessed | tf_op | source)
XLA Modules:
  0.0 548.2 jit_solution(8841497474054207063)
XLA Ops:
  6.5 0.0 all-gather.2.cloned.1.call-start
  6.6 0.7 all-gather.2.cloned.1.call-update
  7.3 0.1 reduce-scatter.2.cloned.1.call-start
  7.4 189.4 %all-gather.2.cloned.1.call-done = bf16[1792,5120]{1,0:T(8,128)(2,1)} async-done(((bf16[224,5120]{1,0:T(8,128)(2,1)}), bf16[1792,5120]{1,0:T(8,128)(2,1)}) %all-gather.2.cloned.1.call-update) | async-done | bytes 18350096 | tf_op jit(solution)/shard_map/all_gather | solution.py:9
  196.8 54.8 %fusion.1 = f32[1792,2176]{1,0:T(8,128)} fusion(bf16[1792,5120]{1,0:T(8,128)(2,1)} %all-gather.2.cloned.1.call-done, bf16[5120,2176]{1,0:T(8,128)(2,1)} %param.5), kind=kOutput, calls=%fused_computation.3 | convolution fusion | flops 39929774080 | bytes 56229888 | tf_op jit(solution)/shard_map/dot_general | solution.py:10
  251.6 56.3 %fusion = bf16[1792,2176]{1,0:T(8,128)(2,1)S(1)} fusion(bf16[1792,5120]{1,0:T(8,128)(2,1)} %all-gather.2.cloned.1.call-done, bf16[5120,2176]{1,0:T(8,128)(2,1)} %param.6, f32[1792,2176]{1,0:T(8,128)} %fusion.1), kind=kOutput, calls=%fused_computation.2 | convolution fusion | flops 39953170432 | bytes 64028672 | tf_op jit(solution)/shard_map/dot_general | solution.py:11
  307.9 49.6 %convolution_convert_fusion = bf16[1792,5120]{1,0:T(8,128)(2,1)} fusion(bf16[1792,2176]{1,0:T(8,128)(2,1)S(1)} %fusion, bf16[2176,5120]{1,0:T(8,128)(2,1)} %param.7), kind=kOutput, calls=%fused_computation | convolution fusion | flops 39938949120 | bytes 48431104 | tf_op jit(solution)/shard_map/dot_general | solution.py:13
  357.5 0.1 reduce-scatter.2.cloned.1.call-update
  357.6 183.8 %reduce-scatter.2.cloned.1.call-done = bf16[224,5120]{1,0:T(8,128)(2,1)} async-done(((bf16[1792,5120]{1,0:T(8,128)(2,1)}), bf16[224,5120]{1,0:T(8,128)(2,1)}) %reduce-scatter.2.cloned.1.call-update) | async-done | bytes 2293776 | tf_op jit(solution)/shard_map/reduce_scatter | solution.py:14
Async XLA Ops:
  6.5 190.2 %all-gather.2.cloned.1.call-start = ((), (), s32[]{:S(2)}) async-start(), calls=%async_computation.1 | async-start | bytes 20643840 | tf_op jit(solution)/shard_map/all_gather | solution.py:9
  7.3 534.1 %reduce-scatter.2.cloned.1.call-start = ((), (), s32[]{:S(2)}) async-start(), calls=%async_computation.2 | async-start | bytes 20643840 | tf_op jit(solution)/shard_map/reduce_scatter | solution.py:14
Sparse Core Ops, SparseCore 0:
  8.9 187.8 all-gather.1
  357.7 183.6 reduce-scatter.1
where the time goes:
time: 549 us; the launch traced here: 548 us
  waiting for transfers between devices  374 us (68%)
  matrix products  161 us (29%)
  between operations  13.4 us (2%)
    all_gather x1, waiting for transfers between devices, step(): rows = lax.all_gather(x, 'tp', axis=0, tiled=True)  189 us
    reduce_scatter x1, waiting for transfers between devices, step(): return lax.psum_scatter(term, 'tp', scatter_dimension=0, tiled=True)  184 us
    dot_general x1, matrix products, step(): up = jnp.dot(rows, w_up, preferred_element_type=jnp.float32)  56.3 us
    dot_general x1, matrix products, step(): gate = jnp.dot(rows, w_gate, preferred_element_type=jnp.float32)  54.8 us
    dot_general x1, matrix products, step(): jnp.dot(hidden, w_down, preferred_element_type=jnp.float32)  49.6 us
  transfers between devices with their start and end apart: 2, of which 2 were waited for; matrix products, arithmetic and copies ran while one was open for 0% of the time, Pallas kernels for 0%

commit v1 on v0

v1 whole, which is shorter than its diff:
```python
import functools

import jax
import jax.numpy as jnp
from jax import lax
from jax.experimental import pallas as pl
from jax.experimental.pallas import tpu as pltpu
from jax.sharding import PartitionSpec as P

LANES = 128
PIECES = 2
SLOTS = 3
TILE = 512
F32 = jnp.float32


def block_kernel(
    n, x_hbm, wg_hbm, wu_hbm, wd_hbm, y_hbm,
    xs, hidden, wtile, wd, arrived, leaving,
    x_sem, w_sem, wd_sem, y_sem, gs_sem, gr_sem, rs_sem, rr_sem, credit,
):
    rows, depth = x_hbm.shape
    units = wd_hbm.shape[0]
    tiles = units // LANES
    half = depth // 2
    chunks = half // TILE
    far = n // 2
    passes = far + 1
    me = lax.axis_index("tp")
    to = (lax.rem(me + 1, n), lax.rem(me + n - 1, n))
    source = (to[1], to[0])
    piece_rows = rows // PIECES

    def slot_of(d, hop):
        return n - 1 if hop == far else 2 * hop - 1 + d

    def piece_of(d, c):
        return c if d == 0 else PIECES - 1 - c

    def gather_copy(d, hop, c):
        at = pl.ds(piece_of(d, c) * piece_rows, piece_rows)
        src = x_hbm.at[at] if hop == 1 else xs.at[slot_of(d, hop - 1), at]
        return pltpu.make_async_remote_copy(
            src_ref=src,
            dst_ref=xs.at[slot_of(d, hop), at],
            send_sem=gs_sem.at[d, hop - 1, c],
            recv_sem=gr_sem.at[d, hop - 1, c],
            device_id={"tp": to[d]},
            device_id_type=pl.DeviceIdType.MESH,
        )

    def pieces_at(hop):
        return PIECES // 2 if hop == far else PIECES

    def receive_and_forward(hop):
        for c in range(pieces_at(hop)):
            for d in (0, 1):
                gather_copy(d, hop, c).wait_recv()
                if hop < far and c < pieces_at(hop + 1):
                    gather_copy(d, hop + 1, c).start()

    def weight_copies(t):
        slot = lax.rem(t, SLOTS)
        cols = pl.ds(pl.multiple_of(lax.rem(t, tiles) * LANES, LANES), LANES)
        return (
            pltpu.make_async_copy(wg_hbm.at[:, cols], wtile.at[slot, :, pl.ds(0, LANES)], w_sem.at[0, slot]),
            pltpu.make_async_copy(wu_hbm.at[:, cols], wtile.at[slot, :, pl.ds(LANES, LANES)], w_sem.at[1, slot]),
        )

    def start_weights(t):
        for copy in weight_copies(t):
            copy.start()

    def gate_up(number, slots, owners):
        def body(j, carry):
            t = number * tiles + j
            for copy in weight_copies(t):
                copy.wait()
            ahead = t + SLOTS - 1

            @pl.when(ahead < passes * tiles)
            def _():
                start_weights(ahead)

            if len(slots) == 1:
                block = xs[slots[0]]
            else:
                block = xs[slots[0] : slots[0] + 2].reshape(2 * rows, depth)
            both = jnp.dot(block, wtile[lax.rem(t, SLOTS)], preferred_element_type=F32)
            h = (jax.nn.silu(both[:, :LANES]) * both[:, LANES:]).astype(jnp.bfloat16)
            cols = pl.ds(pl.multiple_of(j * LANES, LANES), LANES)
            for i, owner in enumerate(owners):
                hidden[owner, :, cols] = h[i * rows : (i + 1) * rows]
            return carry

        lax.fori_loop(0, tiles, body, 0)

    def sum_copy(d, k, c):
        return pltpu.make_async_remote_copy(
            src_ref=leaving.at[d, c],
            dst_ref=arrived.at[d, lax.rem(k, 2), c],
            send_sem=rs_sem.at[d, c],
            recv_sem=rr_sem.at[d, lax.rem(k, 2), c],
            device_id={"tp": to[d]},
            device_id_type=pl.DeviceIdType.MESH,
        )

    def y_copy(d, c):
        cols = pl.ds(pl.multiple_of(d * half + c * TILE, TILE), TILE)
        return pltpu.make_async_copy(xs.at[0, :, cols], y_hbm.at[:, cols], y_sem.at[d, c])

    def sum_step(k, first=False, second=False, ends=False, gives=True):
        def body(c, carry):
            for d in (0, 1):
                owner = lax.rem(k + 1, n) if d == 0 else n - 1 - k
                cols = pl.ds(pl.multiple_of(d * half + c * TILE, TILE), TILE)
                acc = jnp.dot(hidden[owner], wd[:, cols], preferred_element_type=F32)
                if not first:
                    sum_copy(d, k - 1, c).wait_recv()
                    acc = acc + arrived[d, lax.rem(k - 1, 2), c].astype(F32)
                    sum_copy(d, k - 1, c).wait_send()
                if ends:
                    xs[0, :, cols] = acc.astype(jnp.bfloat16)
                else:
                    if not first and not second:
                        pl.semaphore_wait(credit.at[d, c], 1)
                    leaving[d, c] = acc.astype(jnp.bfloat16)
                    if not first and gives:
                        pl.semaphore_signal(
                            credit.at[d, c], inc=1, device_id={"tp": source[d]}, device_id_type=pl.DeviceIdType.MESH
                        )

            @pl.when(c > 0)
            def _():
                for d in (0, 1):
                    (y_copy(d, c - 1) if ends else sum_copy(d, k, c - 1)).start()

            return carry

        lax.fori_loop(0, chunks, body, 0)
        for d in (0, 1):
            (y_copy(d, chunks - 1) if ends else sum_copy(d, k, chunks - 1)).start()

    barrier = pltpu.get_barrier_semaphore()
    for device in to:
        pl.semaphore_signal(barrier, inc=1, device_id={"tp": device}, device_id_type=pl.DeviceIdType.MESH)
    own = pltpu.make_async_copy(x_hbm, xs.at[0], x_sem)
    own.start()
    for t in range(SLOTS - 1):
        start_weights(jnp.int32(t))
    pl.semaphore_wait(barrier, 2)
    for c in range(PIECES):
        for d in (0, 1):
            gather_copy(d, 1, c).start()
    own.wait()
    gate_up(0, (0,), (0,))
    down = pltpu.make_async_copy(wd_hbm, wd, wd_sem)
    down.start()
    for hop in range(1, far):
        receive_and_forward_now = hop < far - 1
        if receive_and_forward_now:
            receive_and_forward(hop)
        else:
            down.wait()
            sum_step(jnp.int32(0), first=True)
            receive_and_forward(hop)
        gate_up(hop, (slot_of(0, hop), slot_of(1, hop)), (hop, n - hop))
    sum_step(jnp.int32(1), second=True)
    receive_and_forward(far)
    gate_up(far, (n - 1,), (far,))

    def middle(k, carry):
        sum_step(k)
        return carry

    lax.fori_loop(2, n - 2, middle, 0)
    sum_step(jnp.int32(n - 2), gives=False)
    sum_step(jnp.int32(n - 1), ends=True)
    for d in (0, 1):
        for hop in range(1, far + 1):
            for c in range(pieces_at(hop)):
                gather_copy(d, hop, c).wait_send()
        for c in range(chunks):
            y_copy(d, c).wait()


def solution(mesh):
    n = mesh.shape["tp"]

    def step(x, w_gate, w_up, w_down):
        rows, depth = x.shape
        units = w_down.shape[0]
        chunks = depth // 2 // TILE
        bf16 = jnp.bfloat16
        dma = pltpu.SemaphoreType.DMA
        return pl.pallas_call(
            functools.partial(block_kernel, n),
            out_shape=jax.ShapeDtypeStruct((rows, depth), bf16),
            in_specs=[pl.BlockSpec(memory_space=pl.ANY)] * 4,
            out_specs=pl.BlockSpec(memory_space=pl.ANY),
            scratch_shapes=[
                pltpu.VMEM((n, rows, depth), bf16),
                pltpu.VMEM((n, rows, units), bf16),
                pltpu.VMEM((SLOTS, depth, 2 * LANES), bf16),
                pltpu.VMEM((units, depth), bf16),
                pltpu.VMEM((2, 2, chunks, rows, TILE), bf16),
                pltpu.VMEM((2, chunks, rows, TILE), bf16),
                dma,
                dma((2, SLOTS)),
                dma,
                dma((2, chunks)),
                dma((2, n // 2, PIECES)),
                dma((2, n // 2, PIECES)),
                dma((2, chunks)),
                dma((2, 2, chunks)),
                pltpu.SemaphoreType.REGULAR((2, chunks)),
            ],
            compiler_params=pltpu.CompilerParams(
                collective_id=0, has_side_effects=True, vmem_limit_bytes=67043328
            ),
            name="mlp_block",
        )(x, w_gate, w_up, w_down)

    return jax.shard_map(
        step,
        mesh=mesh,
        in_specs=(P(("dp", "tp"), None), P(None, "tp"), P(None, "tp"), P("tp", None)),
        out_specs=P(("dp", "tp"), None),
        check_vma=False,
    )
```

time: 549 us -> 359 us (0.65)
  waiting for transfers between devices: 374 us -> 0 us
  Pallas kernels: 0 us -> 356 us
  matrix products: 161 us -> 0 us
  between operations: 13.4 us -> 0.01 us
    pallas_call x0 -> x1, Pallas kernels: none -> 356 us  [step(): pl.pallas_call(functools.partial(block_kernel, n), out_shape=jax.ShapeDty...]
    all_gather x1 -> x0, waiting for transfers between devices: 189 us -> none  [step(): rows = lax.all_gather(x, 'tp', axis=0, tiled=True)]
    reduce_scatter x1 -> x0, waiting for transfers between devices: 184 us -> none  [step(): return lax.psum_scatter(term, 'tp', scatter_dimension=0, tiled=True)]
    dot_general x3 -> x0, matrix products: 161 us -> none  [the longest x1 56.3 us: step(): up = jnp.dot(rows, w_up, preferred_element_type=jnp.float32)]
  transfers between devices with their start and end apart: 2 -> 0, of which waited for: 2 -> 0; matrix products, arithmetic and copies ran while one was open for 0% -> 0% of each run, Pallas kernels for 0% -> 0%
where the time goes in v1:
time: 359 us
  Pallas kernels  356 us (99%)
    pallas_call x1, Pallas kernels, step(): pl.pallas_call(functools.partial(block_kernel, n), out_shape=jax.ShapeDty...  356 us

profile of v1, /device:TPU:22, one launch (start us, length us, event | category | flops | bytes accessed | tf_op | source)
XLA Modules:
  0.0 359.2 jit_solution(1388662519980512658)
XLA Ops:
  0.0 356.1 %mlp_block.1 = bf16[224,5120]{1,0:T(8,128)(2,1)} custom-call(bf16[224,5120]{1,0:T(8,128)(2,1)} %x_hbm.1, bf16[5120,2176]{1,0:T(8,128)(2,1)} %wg_hbm.1, bf16[5120,2176]{1,0:T(8,128)(2,1)} %wu_hbm.1, bf16[2176,5120]{1,0:T(8,128)(2,1)} %wd_hbm.1), custom_call_target="tpu_custom_call" | custom-call | tf_op jit(solution)/shard_map/mlp_block/pallas_call | solution.py:196
  356.1 3.2 copy.6

commit v2 on v1

--- a/solution.py
+++ b/solution.py
@@ -15,9 +15,9 @@
 
 
 def block_kernel(
-    n, x_hbm, wg_hbm, wu_hbm, wd_hbm, y_hbm,
-    xs, hidden, wtile, wd, arrived, leaving,
-    x_sem, w_sem, wd_sem, y_sem, gs_sem, gr_sem, rs_sem, rr_sem, credit,
+    n, x_hbm, wg_hbm, wu_hbm, wd_hbm, y_ref,
+    xs, hidden, wtile, wd, arrived, leaving, term,
+    x_sem, w_sem, wd_sem, gs_sem, gr_sem, rs_sem, rr_sem, credit,
 ):
     rows, depth = x_hbm.shape
     units = wd_hbm.shape[0]
@@ -32,7 +32,7 @@
     piece_rows = rows // PIECES
 
     def slot_of(d, hop):
-        return n - 1 if hop == far else 2 * hop - 1 + d
+        return n - 2 if hop == far else 2 * hop - 2 + d
 
     def piece_of(d, c):
         return c if d == 0 else PIECES - 1 - c
@@ -82,7 +82,9 @@
             def _():
                 start_weights(ahead)
 
-            if len(slots) == 1:
+            if not slots:
+                block = y_ref[...]
+            elif len(slots) == 1:
                 block = xs[slots[0]]
             else:
                 block = xs[slots[0] : slots[0] + 2].reshape(2 * rows, depth)
@@ -105,46 +107,53 @@
             device_id_type=pl.DeviceIdType.MESH,
         )
 
-    def y_copy(d, c):
-        cols = pl.ds(pl.multiple_of(d * half + c * TILE, TILE), TILE)
-        return pltpu.make_async_copy(xs.at[0, :, cols], y_hbm.at[:, cols], y_sem.at[d, c])
-
-    def sum_step(k, first=False, second=False, ends=False, gives=True):
+    def sum_step(k, first=False, second=False, ends=False):
         def body(c, carry):
+            def cols(d):
+                return pl.ds(pl.multiple_of(d * half + c * TILE, TILE), TILE)
+
             for d in (0, 1):
                 owner = lax.rem(k + 1, n) if d == 0 else n - 1 - k
-                cols = pl.ds(pl.multiple_of(d * half + c * TILE, TILE), TILE)
-                acc = jnp.dot(hidden[owner], wd[:, cols], preferred_element_type=F32)
+                term[d] = jnp.dot(hidden[owner], wd[:, cols(d)], preferred_element_type=F32)
+
+            if not ends:
+
+                @pl.when(c > 0)
+                def _():
+                    for d in (0, 1):
+                        sum_copy(d, k, c - 1).start()
+
+            for d in (0, 1):
+                total = term[d]
                 if not first:
                     sum_copy(d, k - 1, c).wait_recv()
-                    acc = acc + arrived[d, lax.rem(k - 1, 2), c].astype(F32)
+                    total = total + arrived[d, lax.rem(k - 1, 2), c].astype(F32)
                     sum_copy(d, k - 1, c).wait_send()
                 if ends:
-                    xs[0, :, cols] = acc.astype(jnp.bfloat16)
+                    y_ref[:, cols(d)] = total.astype(jnp.bfloat16)
                 else:
                     if not first and not second:
                         pl.semaphore_wait(credit.at[d, c], 1)
-                    leaving[d, c] = acc.astype(jnp.bfloat16)
-                    if not first and gives:
-                        pl.semaphore_signal(
-                            credit.at[d, c], inc=1, device_id={"tp": source[d]}, device_id_type=pl.DeviceIdType.MESH
-                        )
-
-            @pl.when(c > 0)
-            def _():
-                for d in (0, 1):
-                    (y_copy(d, c - 1) if ends else sum_copy(d, k, c - 1)).start()
+                    leaving[d, c] = total.astype(jnp.bfloat16)
+                    if not first:
+
+                        @pl.when(k < n - 2)
+                        def _():
+                            pl.semaphore_signal(
+                                credit.at[d, c], inc=1, device_id={"tp": source[d]}, device_id_type=pl.DeviceIdType.MESH
+                            )
 
             return carry
 
         lax.fori_loop(0, chunks, body, 0)
-        for d in (0, 1):
-            (y_copy(d, chunks - 1) if ends else sum_copy(d, k, chunks - 1)).start()
+        if not ends:
+            for d in (0, 1):
+                sum_copy(d, k, chunks - 1).start()
 
     barrier = pltpu.get_barrier_semaphore()
     for device in to:
         pl.semaphore_signal(barrier, inc=1, device_id={"tp": device}, device_id_type=pl.DeviceIdType.MESH)
-    own = pltpu.make_async_copy(x_hbm, xs.at[0], x_sem)
+    own = pltpu.make_async_copy(x_hbm, y_ref, x_sem)
     own.start()
     for t in range(SLOTS - 1):
         start_weights(jnp.int32(t))
@@ -153,7 +162,7 @@
         for d in (0, 1):
             gather_copy(d, 1, c).start()
     own.wait()
-    gate_up(0, (0,), (0,))
+    gate_up(0, (), (0,))
     down = pltpu.make_async_copy(wd_hbm, wd, wd_sem)
     down.start()
     for hop in range(1, far):
@@ -167,21 +176,18 @@
         gate_up(hop, (slot_of(0, hop), slot_of(1, hop)), (hop, n - hop))
     sum_step(jnp.int32(1), second=True)
     receive_and_forward(far)
-    gate_up(far, (n - 1,), (far,))
+    gate_up(far, (n - 2,), (far,))
 
     def middle(k, carry):
         sum_step(k)
         return carry
 
-    lax.fori_loop(2, n - 2, middle, 0)
-    sum_step(jnp.int32(n - 2), gives=False)
+    lax.fori_loop(2, n - 1, middle, 0)
     sum_step(jnp.int32(n - 1), ends=True)
     for d in (0, 1):
         for hop in range(1, far + 1):
             for c in range(pieces_at(hop)):
                 gather_copy(d, hop, c).wait_send()
-        for c in range(chunks):
-            y_copy(d, c).wait()
 
 
 def solution(mesh):
@@ -195,20 +201,20 @@
         dma = pltpu.SemaphoreType.DMA
         return pl.pallas_call(
             functools.partial(block_kernel, n),
-            out_shape=jax.ShapeDtypeStruct((rows, depth), bf16),
+            out_shape=pltpu.VMEM((rows, depth), bf16),
             in_specs=[pl.BlockSpec(memory_space=pl.ANY)] * 4,
-            out_specs=pl.BlockSpec(memory_space=pl.ANY),
+            out_specs=pl.BlockSpec(memory_space=pltpu.VMEM),
             scratch_shapes=[
-                pltpu.VMEM((n, rows, depth), bf16),
+                pltpu.VMEM((n - 1, rows, depth), bf16),
                 pltpu.VMEM((n, rows, units), bf16),
                 pltpu.VMEM((SLOTS, depth, 2 * LANES), bf16),
                 pltpu.VMEM((units, depth), bf16),
                 pltpu.VMEM((2, 2, chunks, rows, TILE), bf16),
                 pltpu.VMEM((2, chunks, rows, TILE), bf16),
+                pltpu.VMEM((2, rows, TILE), F32),
                 dma,
                 dma((2, SLOTS)),
                 dma,
-                dma((2, chunks)),
                 dma((2, n // 2, PIECES)),
                 dma((2, n // 2, PIECES)),
                 dma((2, chunks)),
@@ -216,7 +222,7 @@
                 pltpu.SemaphoreType.REGULAR((2, chunks)),
             ],
             compiler_params=pltpu.CompilerParams(
-                collective_id=0, has_side_effects=True, vmem_limit_bytes=67043328
+                collective_id=0, has_side_effects=True, vmem_limit_bytes=64500000
             ),
             name="mlp_block",
         )(x, w_gate, w_up, w_down)

time: 359 us -> 355 us (0.989)
  no operation moved by 1% of the time
where the time goes in v2:
time: 355 us
  Pallas kernels  354 us (100%)
    pallas_call x1, Pallas kernels, step(): pl.pallas_call(functools.partial(block_kernel, n), out_shape=pltpu.VMEM((...  354 us

profile of v2, /device:TPU:22, one launch (start us, length us, event | category | flops | bytes accessed | tf_op | source)
XLA Modules:
  0.0 354.9 jit_solution(10221527765495982163)
XLA Ops:
  0.0 353.5 %mlp_block.1 = bf16[224,5120]{1,0:T(8,128)(2,1)S(1)} custom-call(bf16[224,5120]{1,0:T(8,128)(2,1)} %x_hbm.1, bf16[5120,2176]{1,0:T(8,128)(2,1)} %wg_hbm.1, bf16[5120,2176]{1,0:T(8,128)(2,1)} %wu_hbm.1, bf16[2176,5120]{1,0:T(8,128)(2,1)} %wd_hbm.1), custom_call_target="tpu_custom_call" | custom-call | tf_op jit(solution)/shard_map/mlp_block/pallas_call | solution.py:202
  353.6 1.4 copy.6

commit v3 on v2

--- a/solution.py
+++ b/solution.py
@@ -10,7 +10,7 @@
 LANES = 128
 PIECES = 2
 SLOTS = 3
-TILE = 512
+TILE = 640
 F32 = jnp.float32
 
 
@@ -128,7 +128,8 @@
                 if not first:
                     sum_copy(d, k - 1, c).wait_recv()
                     total = total + arrived[d, lax.rem(k - 1, 2), c].astype(F32)
-                    sum_copy(d, k - 1, c).wait_send()
+                    if not ends:
+                        sum_copy(d, k - 1, c).wait_send()
                 if ends:
                     y_ref[:, cols(d)] = total.astype(jnp.bfloat16)
                 else:
@@ -146,21 +147,24 @@
             return carry
 
         lax.fori_loop(0, chunks, body, 0)
-        if not ends:
-            for d in (0, 1):
+        for d in (0, 1):
+            if ends:
+                for c in range(chunks):
+                    sum_copy(d, k - 1, c).wait_send()
+            else:
                 sum_copy(d, k, chunks - 1).start()
 
     barrier = pltpu.get_barrier_semaphore()
     for device in to:
         pl.semaphore_signal(barrier, inc=1, device_id={"tp": device}, device_id_type=pl.DeviceIdType.MESH)
+    pl.semaphore_wait(barrier, 2)
+    for c in range(PIECES):
+        for d in (0, 1):
+            gather_copy(d, 1, c).start()
     own = pltpu.make_async_copy(x_hbm, y_ref, x_sem)
     own.start()
     for t in range(SLOTS - 1):
         start_weights(jnp.int32(t))
-    pl.semaphore_wait(barrier, 2)
-    for c in range(PIECES):
-        for d in (0, 1):
-            gather_copy(d, 1, c).start()
     own.wait()
     gate_up(0, (), (0,))
     down = pltpu.make_async_copy(wd_hbm, wd, wd_sem)

time: 355 us -> 355 us (level)
  no operation moved by 1% of the time
where the time goes in v3:
time: 355 us
  Pallas kernels  353 us (99%)
    pallas_call x1, Pallas kernels, step(): pl.pallas_call(functools.partial(block_kernel, n), out_shape=pltpu.VMEM((...  353 us

profile of v3, /device:TPU:22, one launch (start us, length us, event | category | flops | bytes accessed | tf_op | source)
XLA Modules:
  0.0 354.9 jit_solution(5245555528326029558)
XLA Ops:
  0.0 353.5 %mlp_block.1 = bf16[224,5120]{1,0:T(8,128)(2,1)S(1)} custom-call(bf16[224,5120]{1,0:T(8,128)(2,1)} %x_hbm.1, bf16[5120,2176]{1,0:T(8,128)(2,1)} %wg_hbm.1, bf16[5120,2176]{1,0:T(8,128)(2,1)} %wu_hbm.1, bf16[2176,5120]{1,0:T(8,128)(2,1)} %wd_hbm.1), custom_call_target="tpu_custom_call" | custom-call | tf_op jit(solution)/shard_map/mlp_block/pallas_call | solution.py:206
  353.5 1.4 copy.6

commit v4 on v3

--- a/solution.py
+++ b/solution.py
@@ -116,11 +116,12 @@
                 owner = lax.rem(k + 1, n) if d == 0 else n - 1 - k
                 term[d] = jnp.dot(hidden[owner], wd[:, cols(d)], preferred_element_type=F32)
 
-            if not ends:
-
-                @pl.when(c > 0)
-                def _():
-                    for d in (0, 1):
+            @pl.when(c > 0)
+            def _():
+                for d in (0, 1):
+                    if ends:
+                        sum_copy(d, k - 1, c - 1).wait_send()
+                    else:
                         sum_copy(d, k, c - 1).start()
 
             for d in (0, 1):
@@ -149,8 +150,7 @@
         lax.fori_loop(0, chunks, body, 0)
         for d in (0, 1):
             if ends:
-                for c in range(chunks):
-                    sum_copy(d, k - 1, c).wait_send()
+                sum_copy(d, k - 1, chunks - 1).wait_send()
             else:
                 sum_copy(d, k, chunks - 1).start()
 
@@ -187,11 +187,11 @@
         return carry
 
     lax.fori_loop(2, n - 1, middle, 0)
-    sum_step(jnp.int32(n - 1), ends=True)
     for d in (0, 1):
         for hop in range(1, far + 1):
             for c in range(pieces_at(hop)):
                 gather_copy(d, hop, c).wait_send()
+    sum_step(jnp.int32(n - 1), ends=True)
 
 
 def solution(mesh):

time: 355 us -> 355 us (level)
  no operation moved by 1% of the time
where the time goes in v4:
time: 355 us
  Pallas kernels  353 us (99%)
    pallas_call x1, Pallas kernels, step(): pl.pallas_call(functools.partial(block_kernel, n), out_shape=pltpu.VMEM((...  353 us

profile of v4, /device:TPU:22, one launch (start us, length us, event | category | flops | bytes accessed | tf_op | source)
XLA Modules:
  0.0 354.8 jit_solution(17297733189336945248)
XLA Ops:
  0.0 353.4 %mlp_block.1 = bf16[224,5120]{1,0:T(8,128)(2,1)S(1)} custom-call(bf16[224,5120]{1,0:T(8,128)(2,1)} %x_hbm.1, bf16[5120,2176]{1,0:T(8,128)(2,1)} %wg_hbm.1, bf16[5120,2176]{1,0:T(8,128)(2,1)} %wu_hbm.1, bf16[2176,5120]{1,0:T(8,128)(2,1)} %wd_hbm.1), custom_call_target="tpu_custom_call" | custom-call | tf_op jit(solution)/shard_map/mlp_block/pallas_call | solution.py:206
  353.4 1.4 copy.6
